TPU v7x, 32 devices: a whole 2x2x4 slice. The times are simulated.
32 devices in a mesh: node: 4 (over z), local: 8 (over y, x, core).
Axes of the slice: x: 2, y: 2, z: 4, core: 2. Of those that a mesh axis runs over, the one named last changes fastest.
Arguments:
- tokens: bfloat16 [512, 7168], P(('node', 'local')), may hold values from -6 to 6
- grad_out: bfloat16 [512, 7168], P(('node', 'local')), may hold values from -6 to 6
- gates: bfloat16 [512, 3], P(('node', 'local')), may hold values from 0.19921875 to 1
- expert_ids: int32 [512, 3], P(('node', 'local')), may hold values from 0 to 7, as said below
- w_gate: bfloat16 [4, 7168, 2048], P('node', None, 'local'), may hold values from -0.0625 to 0.0625
- w_up: bfloat16 [4, 7168, 2048], P('node', None, 'local'), may hold values from -0.0625 to 0.0625
- w_down: bfloat16 [4, 7168, 2048], P('node', None, 'local'), may hold values from -0.1875 to 0.1875
- s_gate: bfloat16 [7168, 2048], P(None, 'local'), may hold values from -0.0625 to 0.0625
- s_up: bfloat16 [7168, 2048], P(None, 'local'), may hold values from -0.0625 to 0.0625
- s_down: bfloat16 [7168, 2048], P(None, 'local'), may hold values from -0.125 to 0.125
Outputs:
- dx: bfloat16 [512, 7168], P(('node', 'local'))
- dgates: float32 [512, 3], P(('node', 'local'))
- d_w_gate: bfloat16 [4, 7168, 2048], P('node', None, 'local')
- d_w_up: bfloat16 [4, 7168, 2048], P('node', None, 'local')
- d_w_down: bfloat16 [4, 7168, 2048], P('node', None, 'local')
- d_s_gate: bfloat16 [7168, 2048], P('node', 'local')
- d_s_up: bfloat16 [7168, 2048], P('node', 'local')
- d_s_down: bfloat16 [7168, 2048], P('node', 'local')
Inputs may be any that keep to these rules, and one draw needn't show every extreme that they name: `expert_ids`: each token names both experts of one node and one expert of a second node. Of the tokens of one device exactly 8 name experts of each node and at most 8 name any one expert; for every node one of its experts is named by exactly 8 tokens of every device.
All inputs are finite; a program needn't handle non-finite values.
Results may differ from a plain program's by a relative error of at most 0.014.
Values may be sent and summed in bfloat16 or wider, within the bound.
A program may use at most 192 MiB of HBM per device.

v0:
```python
import jax
import jax.numpy as jnp
from jax import lax
from jax.sharding import PartitionSpec as P

E_NODE = 2


precise = lax.Precision.HIGHEST


def silu_parts(pre_gate):
    sig = jax.nn.sigmoid(pre_gate)
    return (pre_gate * sig, sig * (1.0 + pre_gate * (1.0 - sig)))


def contract_first(left, right):
    return lax.dot_general(
        left, right, (((0,), (0,)), ((), ())), preferred_element_type=jnp.float32
    )


def contract_last(left, right):
    return lax.dot_general(
        left, right, (((1,), (1,)), ((), ())), preferred_element_type=jnp.float32
    )


def ffn_backward(rows_in, rows_grad, weight, gate_w, up_w, down_w):
    pre_gate = jnp.dot(rows_in, gate_w, preferred_element_type=jnp.float32)
    pre_up = jnp.dot(rows_in, up_w, preferred_element_type=jnp.float32)
    activ, slope = silu_parts(pre_gate)
    hidden = activ * pre_up
    upstream = jnp.dot(rows_grad, down_w, preferred_element_type=jnp.float32)
    scaled = weight * upstream
    grad_up = (scaled * activ).astype(jnp.bfloat16)
    grad_gate = (scaled * pre_up * slope).astype(jnp.bfloat16)
    weighted = (weight * hidden).astype(jnp.bfloat16)
    return (grad_gate, grad_up, weighted, hidden * upstream)


def expert_work(rows_in, rows_grad, weight, gate_w, up_w, down_w):
    grad_gate, grad_up, weighted, product = ffn_backward(
        rows_in, rows_grad, weight, gate_w, up_w, down_w
    )
    partial_value = (contract_last(grad_gate, gate_w) + contract_last(grad_up, up_w)).astype(
        jnp.bfloat16
    )
    score = jnp.sum(product, axis=1).astype(jnp.bfloat16)
    grads = (
        contract_first(rows_in, grad_gate),
        contract_first(rows_in, grad_up),
        contract_first(rows_grad, weighted),
    )
    return (partial_value, score, grads)


def shared_part(tokens, grad_out, s_gate, s_up, s_down):
    rows_in, rows_grad = (
        lax.all_gather(tokens, "local", axis=0, tiled=True),
        lax.all_gather(grad_out, "local", axis=0, tiled=True),
    )
    unit_weight = jnp.ones((rows_in.shape[0], 1), jnp.float32)
    grad_gate, grad_up, weighted, product = ffn_backward(
        rows_in, rows_grad, unit_weight, s_gate, s_up, s_down
    )
    dx_shared = lax.psum_scatter(
        (contract_last(grad_gate, s_gate) + contract_last(grad_up, s_up)).astype(jnp.bfloat16),
        "local",
        scatter_dimension=0,
        tiled=True,
    ).astype(jnp.float32)
    units = s_gate.shape[1]
    shares = lax.psum_scatter(
        jnp.concatenate(
            [
                contract_first(rows_in, grad_gate),
                contract_first(rows_in, grad_up),
                contract_first(rows_grad, weighted),
            ],
            axis=1,
        ).astype(jnp.bfloat16),
        "node",
        scatter_dimension=0,
        tiled=True,
    ).astype(jnp.float32)
    shared_grads = (
        shares[:, :units].astype(jnp.bfloat16),
        shares[:, units : 2 * units].astype(jnp.bfloat16),
        shares[:, 2 * units :].astype(jnp.bfloat16),
    )
    return (dx_shared, shared_grads)


def routed_part(tokens, grad_out, gates, expert_ids, gate_w, up_w, down_w):
    tokens_here = tokens.shape[0]
    width = tokens.shape[1]
    node_count = lax.axis_size("node")
    local_count = lax.axis_size("local")
    group_size = local_count // E_NODE
    capacity = 2 * tokens_here // node_count
    expert_count = E_NODE * node_count
    slots = jnp.arange(capacity, dtype=jnp.int32)
    chosen = expert_ids[:, :, None] == jnp.arange(expert_count, dtype=jnp.int32)[None, None, :]
    member = jnp.any(chosen, axis=1)
    weight = jnp.sum(jnp.where(chosen, gates.astype(jnp.float32)[:, :, None], 0.0), axis=1)
    ranking = jnp.cumsum(member.astype(jnp.int32), axis=0) - 1
    slot_pick = member[:, :, None] & (ranking[:, :, None] == slots[None, None, :])
    pick_float = slot_pick.astype(jnp.float32)
    slot_gate = jnp.einsum("tes,te->es", pick_float, weight, precision=precise)
    expert_node = jnp.arange(expert_count, dtype=jnp.int32) // E_NODE
    node_ids = jnp.arange(node_count, dtype=jnp.int32)
    node_hit = jnp.any(
        member[:, :, None] & (expert_node[None, :, None] == node_ids[None, None, :]), axis=1
    )
    node_rank = jnp.cumsum(node_hit.astype(jnp.int32), axis=0) - 1
    node_pick = node_hit[:, :, None] & (node_rank[:, :, None] == slots[None, None, :])
    node_rows = node_pick.astype(jnp.bfloat16)
    node_in = jnp.einsum(
        "tnc,td->ncd", node_rows, tokens, preferred_element_type=jnp.float32
    ).astype(jnp.bfloat16)
    node_grad = jnp.einsum(
        "tnc,td->ncd", node_rows, grad_out, preferred_element_type=jnp.float32
    ).astype(jnp.bfloat16)
    expert_pick = jnp.take(node_pick, expert_node, axis=1).astype(jnp.float32)
    select = jnp.einsum("tes,tep->esp", pick_float, expert_pick, precision=precise)
    select = select.reshape(node_count, E_NODE, capacity, capacity).astype(jnp.bfloat16)
    node_gate = slot_gate.reshape(node_count, E_NODE, capacity).astype(jnp.bfloat16)
    got_in, got_grad, got_select, got_gate = (
        lax.all_to_all(node_in, "node", split_axis=0, concat_axis=0, tiled=True),
        lax.all_to_all(node_grad, "node", split_axis=0, concat_axis=0, tiled=True),
        lax.all_to_all(select, "node", split_axis=0, concat_axis=0, tiled=True),
        lax.all_to_all(node_gate, "node", split_axis=0, concat_axis=0, tiled=True),
    )
    routed_in = jnp.einsum(
        "mcsp,mpd->cmsd", got_select, got_in, preferred_element_type=jnp.float32
    ).astype(jnp.bfloat16)
    routed_grad = jnp.einsum(
        "mcsp,mpd->cmsd", got_select, got_grad, preferred_element_type=jnp.float32
    ).astype(jnp.bfloat16)
    routed_gate = jnp.swapaxes(got_gate, 0, 1)

    def spread(values):
        wide = jnp.broadcast_to(values[:, None], (E_NODE, group_size) + values.shape[1:])
        return wide.reshape((local_count,) + values.shape[1:])

    rows_in, rows_grad, rows_gate = (
        lax.all_to_all(spread(routed_in), "local", split_axis=0, concat_axis=0, tiled=True),
        lax.all_to_all(spread(routed_grad), "local", split_axis=0, concat_axis=0, tiled=True),
        lax.all_to_all(spread(routed_gate), "local", split_axis=0, concat_axis=0, tiled=True),
    )
    partial_value, score, grads = expert_work(
        rows_in.reshape(-1, width),
        rows_grad.reshape(-1, width),
        rows_gate.reshape(-1, 1).astype(jnp.float32),
        gate_w,
        up_w,
        down_w,
    )
    back_dx, back_score = (
        lax.all_to_all(
            partial_value.reshape(rows_in.shape), "local", split_axis=0, concat_axis=0, tiled=True
        ),
        lax.all_to_all(
            score.reshape(rows_gate.shape), "local", split_axis=0, concat_axis=0, tiled=True
        ),
    )
    node_sum = jnp.sum(
        back_dx.reshape((E_NODE, group_size) + rows_in.shape[1:]).astype(jnp.float32), axis=1
    )
    score_sum = jnp.sum(
        back_score.reshape((E_NODE, group_size) + rows_gate.shape[1:]).astype(jnp.float32), axis=1
    )
    node_dx = jnp.einsum(
        "mcsp,cmsd->mpd", got_select.astype(jnp.float32), node_sum, precision=precise
    )
    home_dx, home_score = (
        lax.all_to_all(
            node_dx.astype(jnp.bfloat16), "node", split_axis=0, concat_axis=0, tiled=True
        ).astype(node_dx.dtype),
        lax.all_to_all(
            jnp.swapaxes(score_sum, 0, 1).astype(jnp.bfloat16),
            "node",
            split_axis=0,
            concat_axis=0,
            tiled=True,
        ).astype(jnp.float32),
    )
    dx_routed = jnp.einsum("tnc,ncd->td", node_pick.astype(jnp.float32), home_dx, precision=precise)
    slot_score = home_score.reshape(expert_count, capacity)
    token_score = jnp.einsum("tes,es->te", pick_float, slot_score, precision=precise)
    dgates = jnp.sum(jnp.where(chosen, token_score[:, None, :], 0.0), axis=2)
    return (dx_routed, dgates, grads)


def local(tokens, grad_out, gates, expert_ids, w_gate, w_up, w_down, s_gate, s_up, s_down):
    dx_routed, dgates, grads = routed_part(
        tokens, grad_out, gates, expert_ids, w_gate[0], w_up[0], w_down[0]
    )
    dx_shared, shared_grads = shared_part(tokens, grad_out, s_gate, s_up, s_down)
    dx = (dx_routed + dx_shared).astype(jnp.bfloat16)
    expert_grads = tuple((grad.astype(jnp.bfloat16)[None] for grad in grads))
    return (
        dx,
        dgates,
        expert_grads[0],
        expert_grads[1],
        expert_grads[2],
        shared_grads[0],
        shared_grads[1],
        shared_grads[2],
    )


def solution(mesh):
    placed = (
        P(("node", "local"), None),
        P(("node", "local"), None),
        P(("node", "local"), None),
        P(("node", "local"), None),
        P("node", None, "local"),
        P("node", None, "local"),
        P("node", None, "local"),
        P(None, "local"),
        P(None, "local"),
        P(None, "local"),
    )
    return jax.shard_map(
        local,
        mesh=mesh,
        in_specs=placed,
        out_specs=(
            P(("node", "local"), None),
            P(("node", "local"), None),
            P("node", None, "local"),
            P("node", None, "local"),
            P("node", None, "local"),
            P("node", "local"),
            P("node", "local"),
            P("node", "local"),
        ),
        check_vma=False,
    )
```

profile of v0, /device:TPU:0, one launch (start us, length us, event | category | flops | bytes accessed | tf_op | source)
XLA Modules:
  0.0 373.8 jit_solution(17116785082330466445)
XLA Ops:
  8.7 30.6 %all-gather.5.cloned.1.call-done = bf16[128,7168]{1,0:T(8,128)(2,1)} async-done(((bf16[16,7168]{1,0:T(8,128)(2,1)}), bf16[128,7168]{1,0:T(8,128)(2,1)}) %all-gather.5.cloned.1.call-update) | async-done | bytes 1835024 | tf_op jit(solution)/shard_map/all_gather | solution.py:60
  39.3 3.4 fusion.59
  44.2 23.7 %all-gather.3.cloned.1.call-done = bf16[128,7168]{1,0:T(8,128)(2,1)} async-done(((bf16[16,7168]{1,0:T(8,128)(2,1)}), bf16[128,7168]{1,0:T(8,128)(2,1)}) %all-gather.3.cloned.1.call-update) | async-done | bytes 1835024 | tf_op jit(solution)/shard_map/all_gather | solution.py:61
  67.9 3.4 multiply_convert_fusion.5
  73.6 2.6 fusion.7
  80.0 10.9 %pad_maximum_fusion = bf16[7168,768]{0,1:T(8,128)(2,1)} fusion(bf16[7168,256]{0,1:T(8,128)(2,1)S(1)} %fusion.6, bf16[7168,256]{0,1:T(8,128)(2,1)S(1)} %fusion.5, bf16[7168,256]{0,1:T(8,128)(2,1)S(1)} %fusion.4), kind=kLoop, calls=%fused_computation.1 | loop fusion | flops 33030144 | bytes 22020096 | tf_op jit(solution)/shard_map/concatenate | solution.py:75
  93.5 4.6 %all-to-all-start = ((bf16[4,2,8,8]{3,2,1,0:T(8,128)(2,1)}), bf16[4,2,8,8]{3,2,1,0:T(8,128)(2,1)S(1)}, u32[]{:S(2)}, u32[]{:S(2)}) async-start(bf16[4,2,8,8]{3,2,1,0:T(8,128)(2,1)} %bitcast.2), calls=%async_computation | async-start | bytes 32768 | tf_op jit(solution)/shard_map/all_to_all | solution.py:132
  99.2 4.6 %all-to-all-done = bf16[4,2,8,8]{3,2,1,0:T(8,128)(2,1)S(1)} async-done(((bf16[4,2,8,8]{3,2,1,0:T(8,128)(2,1)}), bf16[4,2,8,8]{3,2,1,0:T(8,128)(2,1)S(1)}, u32[]{:S(2)}, u32[]{:S(2)}) %all-to-all-start) | async-done | bytes 1056 | tf_op jit(solution)/shard_map/all_to_all | solution.py:132
  103.8 3.5 all-to-all-start.5
  108.3 11.3 %all-to-all-done.5 = bf16[4,8,7168]{2,1,0:T(8,128)(2,1)S(1)} async-done(((bf16[4,8,7168]{2,1,0:T(8,128)(2,1)}), bf16[4,8,7168]{2,1,0:T(8,128)(2,1)S(1)}, u32[]{:S(2)}, u32[]{:S(2)}) %all-to-all-start.5) | async-done | bytes 458784 | tf_op jit(solution)/shard_map/all_to_all | solution.py:130
  119.5 3.5 all-to-all-start.3
  123.5 24.4 %all-to-all-done.3 = bf16[4,8,7168]{2,1,0:T(8,128)(2,1)S(1)} async-done(((bf16[4,8,7168]{2,1,0:T(8,128)(2,1)}), bf16[4,8,7168]{2,1,0:T(8,128)(2,1)S(1)}, u32[]{:S(2)}, u32[]{:S(2)}) %all-to-all-start.3) | async-done | bytes 458784 | tf_op jit(solution)/shard_map/all_to_all | solution.py:131
  147.9 2.3 broadcast_in_dim.78
  150.2 4.5 %all-to-all-start.6 = ((bf16[8,4,8,7168]{3,2,1,0:T(8,128)(2,1)}), bf16[8,4,8,7168]{3,2,1,0:T(8,128)(2,1)}, u32[]{:S(2)}, u32[]{:S(2)}) async-start(bf16[8,4,8,7168]{3,2,1,0:T(8,128)(2,1)} %bitcast.121), calls=%async_computation.6 | async-start | bytes 7340032 | tf_op jit(solution)/shard_map/all_to_all | solution.py:148
  155.2 43.0 %all-to-all-done.6 = bf16[8,4,8,7168]{3,2,1,0:T(8,128)(2,1)} async-done(((bf16[8,4,8,7168]{3,2,1,0:T(8,128)(2,1)}), bf16[8,4,8,7168]{3,2,1,0:T(8,128)(2,1)}, u32[]{:S(2)}, u32[]{:S(2)}) %all-to-all-start.6) | async-done | bytes 3670048 | tf_op jit(solution)/shard_map/all_to_all | solution.py:148
  198.2 2.3 broadcast_in_dim.49
  200.5 4.7 %all-to-all-start.4 = ((bf16[8,4,8,7168]{3,2,1,0:T(8,128)(2,1)}), bf16[8,4,8,7168]{3,2,1,0:T(8,128)(2,1)}, u32[]{:S(2)}, u32[]{:S(2)}) async-start(bf16[8,4,8,7168]{3,2,1,0:T(8,128)(2,1)} %bitcast.122), calls=%async_computation.4 | async-start | bytes 7340032 | tf_op jit(solution)/shard_map/all_to_all | solution.py:149
  205.2 5.1 %fusion.15 = f32[256,256]{0,1:T(8,128)S(1)} fusion(bf16[256,7168]{1,0:T(8,128)(2,1)} %bitcast.22, bf16[1,7168,256]{2,1,0:T(8,128)(2,1)} %param.14), kind=kOutput, calls=%fused_computation.32 | convolution fusion | flops 939524096 | bytes 7602176 | tf_op jit(solution)/shard_map/dot_general | solution.py:30
  210.3 3.7 fusion.18
  214.0 34.5 %all-to-all-done.4 = bf16[8,4,8,7168]{3,2,1,0:T(8,128)(2,1)} async-done(((bf16[8,4,8,7168]{3,2,1,0:T(8,128)(2,1)}), bf16[8,4,8,7168]{3,2,1,0:T(8,128)(2,1)}, u32[]{:S(2)}, u32[]{:S(2)}) %all-to-all-start.4) | async-done | bytes 3670048 | tf_op jit(solution)/shard_map/all_to_all | solution.py:149
  248.5 4.7 %multiply_reduce_fusion = (bf16[256]{0:T(256)(128)(2,1)S(1)}, f32[256,256]{0,1:T(8,128)S(1)}) fusion(f32[256,256]{0,1:T(8,128)S(1)} %fusion.18, f32[256,256]{0,1:T(8,128)S(1)} %fusion.15, bf16[256,7168]{1,0:T(8,128)(2,1)} %bitcast.15, bf16[1,7168,256]{2,1,0:T(8,128)(2,1)} %param.16), kind=kOutput, calls=%fused_computation.44 | convolution fusion | flops 939982592 | bytes 8126976 | tf_op jit(solution)/shard_map/dot_general | solution.py:34
  253.3 7.1 %all_to_all.55 = bf16[8,4,8]{2,1,0:T(4,128)(2,1)S(1)} all-to-all(bf16[8,4,8]{2,1,0:T(4,128)(2,1)S(1)} %convert_element_type.164), channel_id=1, replica_groups=mesh['node'=4,'local'=8] {'local'}, dimensions={0} | all-to-all | bytes 1024 | tf_op jit(solution)/shard_map/all_to_all | solution.py:164
  261.0 3.2 all-to-all-start.10
  264.2 7.3 %all-to-all-done.10 = bf16[4,2,8]{2,1,0:T(2,128)(2,1)S(1)} async-done(((bf16[4,2,8]{2,1,0:T(2,128)(2,1)}), bf16[4,2,8]{2,1,0:T(2,128)(2,1)S(1)}, u32[]{:S(2)}, u32[]{:S(2)}) %all-to-all-start.10) | async-done | bytes 160 | tf_op jit(solution)/shard_map/all_to_all | solution.py:181
  272.4 8.1 %all_to_all.56 = bf16[4,2,8]{2,1,0:T(2,128)(2,1)S(1)} all-to-all(bf16[4,2,8]{2,1,0:T(2,128)(2,1)S(1)} %bitcast.125), channel_id=1, replica_groups=mesh['node'=4,'local'=8] {'node'}, dimensions={0} | all-to-all | bytes 256 | tf_op jit(solution)/shard_map/all_to_all | solution.py:133
  280.5 7.3 %all_to_all.57 = bf16[8,4,8]{2,1,0:T(4,128)(2,1)S(1)} all-to-all(bf16[8,4,8]{2,1,0:T(4,128)(2,1)S(1)} %bitcast.123), channel_id=1, replica_groups=mesh['node'=4,'local'=8] {'local'}, dimensions={0} | all-to-all | bytes 1024 | tf_op jit(solution)/shard_map/all_to_all | solution.py:150
  288.0 3.5 fusion.13
  292.6 45.9 %all_to_all.58 = bf16[8,4,8,7168]{3,2,1,0:T(8,128)(2,1)S(1)} all-to-all(bf16[8,4,8,7168]{3,2,1,0:T(8,128)(2,1)S(1)} %bitcast.120), channel_id=1, replica_groups=mesh['node'=4,'local'=8] {'local'}, dimensions={0} | all-to-all | bytes 7340032 | tf_op jit(solution)/shard_map/all_to_all | solution.py:161
  340.6 3.8 %all-to-all-start.8 = ((bf16[4,8,7168]{2,1,0:T(8,128)(2,1)}), bf16[4,8,7168]{2,1,0:T(8,128)(2,1)S(1)}, u32[]{:S(2)}, u32[]{:S(2)}) async-start(bf16[4,8,7168]{2,1,0:T(8,128)(2,1)} %fusion.10), calls=%async_computation.8 | async-start | bytes 917504 | tf_op jit(solution)/shard_map/all_to_all | solution.py:178
  344.4 5.1 %fusion.1 = bf16[1,7168,256]{2,1,0:T(8,128)(2,1)} fusion(bf16[256,7168]{1,0:T(8,128)(2,1)} %bitcast.22, bf16[256,256]{0,1:T(8,128)(2,1)S(1)} %get-tuple-element.46), kind=kOutput, calls=%fused_computation.10 | convolution fusion | flops 941359104 | bytes 7471104 | tf_op jit(solution)/shard_map/dot_general | solution.py:18
  349.4 5.0 %fusion.2 = bf16[1,7168,256]{2,1,0:T(8,128)(2,1)} fusion(bf16[256,7168]{1,0:T(8,128)(2,1)} %bitcast.22, bf16[256,256]{0,1:T(8,128)(2,1)S(1)} %get-tuple-element.45), kind=kOutput, calls=%fused_computation.11 | convolution fusion | flops 941359104 | bytes 7471104 | tf_op jit(solution)/shard_map/dot_general | solution.py:18
  354.5 5.1 %fusion.3 = bf16[1,7168,256]{2,1,0:T(8,128)(2,1)} fusion(bf16[256,7168]{1,0:T(8,128)(2,1)} %bitcast.15, f32[256]{0:T(256)S(1)} %reshape.177, f32[256,256]{0,1:T(8,128)S(1)} %fusion.18, f32[256,256]{0,1:T(8,128)S(1)} %fusion.15), kind=kOutput, calls=%fused_computation.12 | convolution fusion | flops 941817856 | bytes 7865344 | tf_op jit(solution)/shard_map/dot_general | solution.py:18
  (84 shorter events, 27.4 us)
Async XLA Ops:
  7.2 32.1 %all-gather.5.cloned.1.call-start = ((), (), s32[]{:S(2)}) async-start(), calls=%async_computation.14 | async-start | bytes 2064384 | tf_op jit(solution)/shard_map/all_gather | solution.py:60
  7.9 60.0 %all-gather.3.cloned.1.call-start = ((), (), s32[]{:S(2)}) async-start(), calls=%async_computation.13 | async-start | bytes 2064384 | tf_op jit(solution)/shard_map/all_gather | solution.py:61
  8.6 350.9 %reduce-scatter.3.cloned.1.call-start = ((), (), s32[]{:S(2)}) async-start(), calls=%async_computation.15 | async-start | bytes 2064384 | tf_op jit(solution)/shard_map/reduce_scatter | solution.py:67
  39.3 3.4 copy-start
  39.3 4.2 %copy-start.3 = (bf16[7168,256]{1,0:T(8,128)(2,1)S(1)}, bf16[7168,256]{1,0:T(8,128)(2,1)}, u32[]{:S(2)}) copy-start(bf16[7168,256]{1,0:T(8,128)(2,1)} %param.17) | copy-start | bytes 11010052
  67.9 3.7 copy-start.4
  71.6 2.0 copy-start.5
  76.2 285.3 %reduce-scatter.5.cloned.1.call-start = ((), (), s32[]{:S(2)}) async-start(), calls=%async_computation.16 | async-start | bytes 13762560 | tf_op jit(solution)/shard_map/reduce_scatter | solution.py:74
  77.4 1.5 copy-start.6
  90.9 0.7 copy-start.9
  90.9 7.2 %copy-start.7 = (bf16[16,7168]{1,0:T(8,128)(2,1)S(1)}, bf16[16,7168]{1,0:T(8,128)(2,1)}, u32[]{:S(2)}) copy-start(bf16[16,7168]{1,0:T(8,128)(2,1)} %param.10) | copy-start | bytes 688132
  90.9 16.3 %copy-start.8 = (bf16[16,7168]{1,0:T(8,128)(2,1)S(1)}, bf16[16,7168]{1,0:T(8,128)(2,1)}, u32[]{:S(2)}) copy-start(bf16[16,7168]{1,0:T(8,128)(2,1)} %param.11) | copy-start | bytes 688132
  93.5 10.2 %all-to-all-start = ((bf16[4,2,8,8]{3,2,1,0:T(8,128)(2,1)}), bf16[4,2,8,8]{3,2,1,0:T(8,128)(2,1)S(1)}, u32[]{:S(2)}, u32[]{:S(2)}) async-start(bf16[4,2,8,8]{3,2,1,0:T(8,128)(2,1)} %bitcast.2), calls=%async_computation | async-start | bytes 32768 | tf_op jit(solution)/shard_map/all_to_all | solution.py:132
  103.8 15.8 %all-to-all-start.5 = ((bf16[4,8,7168]{2,1,0:T(8,128)(2,1)}), bf16[4,8,7168]{2,1,0:T(8,128)(2,1)S(1)}, u32[]{:S(2)}, u32[]{:S(2)}) async-start(bf16[4,8,7168]{2,1,0:T(8,128)(2,1)} %convolution_convert_fusion.8), calls=%async_computation.5 | async-start | bytes 917504 | tf_op jit(solution)/shard_map/all_to_all | solution.py:130
  119.5 28.4 %all-to-all-start.3 = ((bf16[4,8,7168]{2,1,0:T(8,128)(2,1)}), bf16[4,8,7168]{2,1,0:T(8,128)(2,1)S(1)}, u32[]{:S(2)}, u32[]{:S(2)}) async-start(bf16[4,8,7168]{2,1,0:T(8,128)(2,1)} %convolution_convert_fusion.9), calls=%async_computation.3 | async-start | bytes 917504 | tf_op jit(solution)/shard_map/all_to_all | solution.py:131
  150.2 48.0 %all-to-all-start.6 = ((bf16[8,4,8,7168]{3,2,1,0:T(8,128)(2,1)}), bf16[8,4,8,7168]{3,2,1,0:T(8,128)(2,1)}, u32[]{:S(2)}, u32[]{:S(2)}) async-start(bf16[8,4,8,7168]{3,2,1,0:T(8,128)(2,1)} %bitcast.121), calls=%async_computation.6 | async-start | bytes 7340032 | tf_op jit(solution)/shard_map/all_to_all | solution.py:148
  200.5 48.0 %all-to-all-start.4 = ((bf16[8,4,8,7168]{3,2,1,0:T(8,128)(2,1)}), bf16[8,4,8,7168]{3,2,1,0:T(8,128)(2,1)}, u32[]{:S(2)}, u32[]{:S(2)}) async-start(bf16[8,4,8,7168]{3,2,1,0:T(8,128)(2,1)} %bitcast.122), calls=%async_computation.4 | async-start | bytes 7340032 | tf_op jit(solution)/shard_map/all_to_all | solution.py:149
  205.2 5.1 %copy-start.1 = (bf16[1,7168,256]{2,1,0:T(8,128)(2,1)S(1)}, bf16[1,7168,256]{2,1,0:T(8,128)(2,1)}, u32[]{:S(2)}) copy-start(bf16[1,7168,256]{2,1,0:T(8,128)(2,1)} %param.15) | copy-start | bytes 11010052
  248.5 15.7 %copy-start.10 = (bf16[16,3]{0,1:T(4,128)(2,1)S(1)}, bf16[16,3]{0,1:T(4,128)(2,1)}, u32[]{:S(2)}) copy-start(bf16[16,3]{0,1:T(4,128)(2,1)} %param.12) | copy-start | bytes 292
  261.0 10.5 %all-to-all-start.10 = ((bf16[4,2,8]{2,1,0:T(2,128)(2,1)}), bf16[4,2,8]{2,1,0:T(2,128)(2,1)S(1)}, u32[]{:S(2)}, u32[]{:S(2)}) async-start(bf16[4,2,8]{2,1,0:T(2,128)(2,1)} %copy.62), calls=%async_computation.11 | async-start | bytes 4096 | tf_op jit(solution)/shard_map/all_to_all | solution.py:181
  288.0 3.5 copy-start.2
  340.6 18.9 %all-to-all-start.8 = ((bf16[4,8,7168]{2,1,0:T(8,128)(2,1)}), bf16[4,8,7168]{2,1,0:T(8,128)(2,1)S(1)}, u32[]{:S(2)}, u32[]{:S(2)}) async-start(bf16[4,8,7168]{2,1,0:T(8,128)(2,1)} %fusion.10), calls=%async_computation.8 | async-start | bytes 917504 | tf_op jit(solution)/shard_map/all_to_all | solution.py:178
Sparse Core Ops, SparseCore 0:
  9.9 29.3 all-gather.4
  41.2 26.6 all-gather.2
  76.3 39.5 reduce-scatter.2
  118.1 192.6 reduce-scatter.4
where the time goes:
time: 375 us; the launch traced here: 374 us
  waiting for transfers between devices  181 us (48%)
  blocking collectives  68.3 us (18%)
  matrix products  55.4 us (15%)
  starting transfers between devices  27.8 us (7%)
  local copies, waits for them, and re-layouts  15 us (4%)
  between operations  14.1 us (4%)
  other arithmetic  12.4 us (3%)
    all_to_all x1, blocking collectives, routed_part(): lax.all_to_all(partial_value.reshape(rows_in.shape), 'local', split_axis=...  45.9 us
    all_to_all x1, waiting for transfers between devices, routed_part(): lax.all_to_all(spread(routed_in), 'local', split_axis=0, concat_axis=0, t...  43 us
    all_to_all x1, waiting for transfers between devices, routed_part(): lax.all_to_all(spread(routed_grad), 'local', split_axis=0, concat_axis=0,...  34.5 us
    all_gather x1, waiting for transfers between devices, shared_part(): lax.all_gather(tokens, 'local', axis=0, tiled=True)  30.6 us
    all_to_all x1, waiting for transfers between devices, routed_part(): lax.all_to_all(node_grad, 'node', split_axis=0, concat_axis=0, tiled=True)  24.4 us
    all_gather x1, waiting for transfers between devices, shared_part(): lax.all_gather(grad_out, 'local', axis=0, tiled=True)  23.7 us
    dot_general x6, matrix products, contract_first(): lax.dot_general(left, right, (((0,), (0,)), ((), ())), preferred_element_...  18.6 us
    all_to_all x1, waiting for transfers between devices, routed_part(): lax.all_to_all(node_in, 'node', split_axis=0, concat_axis=0, tiled=True)  11.3 us
  transfers between devices with their start and end apart: 11, of which 8 were waited for; matrix products, arithmetic and copies ran while one was open for 18% of the time, Pallas kernels for 0%

commit v1 on v0

v1 whole, which is shorter than its diff:
```python
import functools

import jax
import jax.numpy as jnp
from jax import lax
from jax.experimental import pallas as pl
from jax.experimental.pallas import tpu as pltpu
from jax.sharding import PartitionSpec as P

E_NODE = 2
LANES = 128
MESH = pl.DeviceIdType.MESH


def bit_orders(local_count):
    bits = local_count.bit_length() - 1
    outer = list(range(1, bits))
    forward = [1 << b for b in outer] + [1]
    backward = [1 << b for b in outer[::-1]] + [1]
    return (forward, backward)


def near_first(node_count):
    return sorted(range(1, node_count), key=lambda s: min(s, node_count - s))


def greet(node_count, masks):
    n, l = lax.axis_index("node"), lax.axis_index("local")
    barrier = pltpu.get_barrier_semaphore()
    for r in range(1, node_count):
        pl.semaphore_signal(
            barrier, inc=1, device_id=(lax.rem(n + r, node_count), l), device_id_type=MESH
        )
    for mask in masks:
        pl.semaphore_signal(barrier, inc=1, device_id=(n, l ^ mask), device_id_type=MESH)
    pl.semaphore_wait(barrier, node_count - 1 + len(masks))


def gather_kernel(
    node_count, orders, tok, grad, sel_t, sel_g, meta,
    all_t, all_g, ext_t, ext_g, all_m, send_sem, recv_sem, own_sem,
):
    n, l = lax.axis_index("node"), lax.axis_index("local")
    forward, backward = orders
    stages = len(forward)
    own_blocks = tok.shape[0]
    part = ext_t.shape[-1]
    greet(node_count, forward)
    counter = [0]
    sends = []

    def remote(src, dst, device):
        i = counter[0]
        counter[0] += 1
        copy = pltpu.make_async_remote_copy(
            src_ref=src, dst_ref=dst, send_sem=send_sem.at[i], recv_sem=recv_sem.at[i],
            device_id=device, device_id_type=MESH,
        )
        copy.start()
        sends.append(copy)
        return copy

    fills = [
        pltpu.make_async_copy(tok, all_t.at[0, pl.ds(0, own_blocks)], own_sem.at[0]),
        pltpu.make_async_copy(grad, all_g.at[0, pl.ds(0, own_blocks)], own_sem.at[1]),
        pltpu.make_async_copy(meta.at[0], all_m.at[0, 0], own_sem.at[2]),
    ]
    for fill in fills:
        fill.start()

    def view(buf, s, start, size):
        if buf is all_t or buf is all_g:
            if s == 0:
                return buf.at[pl.ds(start, size), pl.ds(0, own_blocks)]
            return buf.at[pl.ds(start, size), own_blocks + s - 1]
        if buf is all_m:
            return buf.at[s, pl.ds(start, size)]
        return buf.at[s - 1, pl.ds(start, size)]

    arrived = {}
    order = near_first(node_count)
    for s in order:
        r = node_count - s
        m = lax.rem(n + r, node_count)
        columns = pl.ds(pl.multiple_of(m * part, LANES), part)
        arrived[s] = [
            remote(meta.at[r], all_m.at[s, 0], (m, l)),
            remote(sel_t.at[r - 1], all_t.at[0, own_blocks + s - 1], (m, l)),
            remote(sel_g.at[r - 1], all_g.at[0, own_blocks + s - 1], (m, l)),
            remote(tok.at[:, :, columns], ext_t.at[s - 1, 0], (m, l)),
            remote(grad.at[:, :, columns], ext_g.at[s - 1, 0], (m, l)),
        ]
    for fill in fills:
        fill.wait()

    items = [0] + order
    pending = {}

    def issue(item, stage):
        s = items[item]
        bufs = [(all_m, forward), (all_t, forward), (all_g, backward)]
        if s > 0:
            bufs += [(ext_t, forward), (ext_g, backward)]
        if stage > 0:
            before = pending[item]
        else:
            before = arrived.get(s, [])
        for copy in before:
            copy.wait_recv()
        size = 1 << stage
        pending[item] = [
            remote(view(buf, s, 0, size), view(buf, s, size, size), (n, l ^ bits[stage]))
            for buf, bits in bufs
        ]

    for tick in range(len(items) + stages - 1):
        for item in range(len(items)):
            stage = tick - item
            if 0 <= stage < stages:
                issue(item, stage)
    for item in range(len(items)):
        for copy in pending[item]:
            copy.wait_recv()
    for copy in sends:
        copy.wait_send()


def gather_rows(node_count, local_count, tok, grad, sel_t, sel_g, meta):
    own_blocks, cap, width = tok.shape
    orders = bit_orders(local_count)
    part = width // node_count
    copies = len(orders[0]) * (3 + 5 * (node_count - 1)) + 5 * (node_count - 1)
    rows = (local_count, own_blocks + node_count - 1, cap, width)
    ext = (node_count - 1, local_count, own_blocks, cap, part)
    bf16 = jnp.bfloat16
    vmem = pl.BlockSpec(memory_space=pltpu.VMEM)
    hbm = pl.BlockSpec(memory_space=pl.ANY)
    return pl.pallas_call(
        functools.partial(gather_kernel, node_count, orders),
        out_shape=[
            jax.ShapeDtypeStruct(rows, bf16),
            jax.ShapeDtypeStruct(rows, bf16),
            jax.ShapeDtypeStruct(ext, bf16),
            jax.ShapeDtypeStruct(ext, bf16),
            jax.ShapeDtypeStruct((node_count, local_count) + meta.shape[1:], bf16),
        ],
        in_specs=[vmem] * 5,
        out_specs=[hbm] * 5,
        scratch_shapes=[
            pltpu.SemaphoreType.DMA((copies,)),
            pltpu.SemaphoreType.DMA((copies,)),
            pltpu.SemaphoreType.DMA((3,)),
        ],
        compiler_params=pltpu.CompilerParams(collective_id=0, has_side_effects=True),
        name="gather_rows",
    )(tok, grad, sel_t, sel_g, meta)


def reduce_kernel(node_count, forward, own_blocks, part_ref, own_ref, home_ref,
                  acc, land, back, send_sem, recv_sem, zsend_sem, zrecv_sem, load_sem):
    n, l = lax.axis_index("node"), lax.axis_index("local")
    count, blocks, cap, width = part_ref.shape
    stages = len(forward)
    half = width // 2 // LANES * LANES
    load = pltpu.make_async_copy(part_ref, acc, load_sem)
    load.start()
    greet(node_count, forward)
    load.wait()
    groups = [(own_blocks, blocks - own_blocks), (0, own_blocks)]
    bands = [(0, half), (half, width - half)]
    top = stages - 1
    plans = [[top] + list(range(top))[::-1], [top] + list(range(top))]
    counter = [0]
    sends = []
    keep = {key: list(range(count)) for key in [(g, b) for g in range(2) for b in range(2)]}
    flight = {}

    def start(g, b, stage):
        bit = 1 << plans[b][stage]
        first, size = groups[g]
        columns = pl.ds(*bands[b])
        out = [p for p in keep[g, b] if p & bit]
        stay = [p for p in keep[g, b] if not p & bit]
        keep[g, b] = stay
        copies = []
        for p in out:
            i = counter[0]
            counter[0] += 1
            copy = pltpu.make_async_remote_copy(
                src_ref=acc.at[p, pl.ds(first, size), :, columns],
                dst_ref=land.at[p, pl.ds(first, size), :, columns],
                send_sem=send_sem.at[i], recv_sem=recv_sem.at[i],
                device_id=(n, l ^ forward[plans[b][stage]]), device_id_type=MESH,
            )
            copy.start()
            sends.append(copy)
            copies.append((p, copy))
        flight[g, b] = (bit, copies)

    def settle(g, b):
        first, size = groups[g]
        columns = pl.ds(*bands[b])
        bit, copies = flight[g, b]
        for p, copy in copies:
            copy.wait_recv()
            q = p ^ bit

            def add(k, carry, p=p, q=q):
                there = land[p, first + k, :, columns].astype(jnp.float32)
                here = acc[q, first + k, :, columns].astype(jnp.float32)
                acc[q, first + k, :, columns] = (here + there).astype(jnp.bfloat16)
                return carry

            lax.fori_loop(0, size, add, 0)

    homes = []
    for stage in range(stages + 1):
        for g in range(2):
            for b in range(2):
                if stage > 0:
                    settle(g, b)
                if stage < stages:
                    start(g, b, stage)
            if stage == stages and g == 0:
                for s in near_first(node_count):
                    copy = pltpu.make_async_remote_copy(
                        src_ref=acc.at[0, own_blocks + s - 1],
                        dst_ref=back.at[node_count - s - 1],
                        send_sem=zsend_sem.at[s - 1],
                        recv_sem=zrecv_sem.at[node_count - s - 1],
                        device_id=(lax.rem(n + s, node_count), l), device_id_type=MESH,
                    )
                    copy.start()
                    homes.append(copy)
    own_ref[...] = acc[0, pl.ds(0, own_blocks)]
    for copy in homes:
        copy.wait_recv()
    home_ref[...] = back[...]
    for copy in sends + homes:
        copy.wait_send()


def reduce_rows(node_count, local_count, part):
    count, blocks, cap, width = part.shape
    forward = bit_orders(local_count)[0]
    own_blocks = blocks - (node_count - 1)
    bf16 = jnp.bfloat16
    vmem = pl.BlockSpec(memory_space=pltpu.VMEM)
    copies = 4 * (local_count - 1)
    return pl.pallas_call(
        functools.partial(reduce_kernel, node_count, forward, own_blocks),
        out_shape=[
            jax.ShapeDtypeStruct((own_blocks, cap, width), bf16),
            jax.ShapeDtypeStruct((node_count - 1, cap, width), bf16),
        ],
        in_specs=[pl.BlockSpec(memory_space=pl.ANY)],
        out_specs=[vmem] * 2,
        scratch_shapes=[
            pltpu.VMEM(part.shape, bf16),
            pltpu.VMEM(part.shape, bf16),
            pltpu.VMEM((node_count - 1, cap, width), bf16),
            pltpu.SemaphoreType.DMA((copies,)),
            pltpu.SemaphoreType.DMA((copies,)),
            pltpu.SemaphoreType.DMA((node_count - 1,)),
            pltpu.SemaphoreType.DMA((node_count - 1,)),
            pltpu.SemaphoreType.DMA,
        ],
        compiler_params=pltpu.CompilerParams(collective_id=1, has_side_effects=True),
        name="reduce_rows",
    )(part)


def silu_parts(pre_gate):
    sig = jax.nn.sigmoid(pre_gate)
    return (pre_gate * sig, sig * (1.0 + pre_gate * (1.0 - sig)))


def dot(left, right):
    return jnp.dot(left, right, preferred_element_type=jnp.float32)


def contract_first(left, right):
    return lax.dot_general(
        left, right, (((0,), (0,)), ((), ())), preferred_element_type=jnp.float32
    )


def contract_last(left, right):
    return lax.dot_general(
        left, right, (((1,), (1,)), ((), ())), preferred_element_type=jnp.float32
    )


def flip(values, local_count):
    bits = local_count.bit_length() - 1
    shaped = values.reshape((2,) * bits + (-1,) + values.shape[1:])
    axes = (0,) + tuple(range(1, bits))[::-1] + tuple(range(bits, shaped.ndim))
    return jnp.transpose(shaped, axes).reshape(values.shape)


def ffn_backward(pre_gate, pre_up, upstream, weight):
    activ, slope = silu_parts(pre_gate)
    hidden = activ * pre_up
    scaled = weight * upstream
    grad_up = (scaled * activ).astype(jnp.bfloat16)
    grad_gate = (scaled * pre_up * slope).astype(jnp.bfloat16)
    weighted = (weight * hidden).astype(jnp.bfloat16)
    return (grad_gate, grad_up, weighted, hidden * upstream)


def local(tokens, grad_out, gates, expert_ids, w_gate, w_up, w_down, s_gate, s_up, s_down):
    held, width = tokens.shape
    nodes, locals_ = lax.axis_size("node"), lax.axis_size("local")
    n, l = lax.axis_index("node"), lax.axis_index("local")
    cap = 2 * held // nodes
    own_blocks = held // cap
    bf16, f32 = jnp.bfloat16, jnp.float32

    rel = lax.rem(expert_ids // E_NODE - n + nodes, nodes)
    near = jnp.arange(nodes, dtype=jnp.int32)
    hit_k = rel[:, :, None] == near
    hit = jnp.any(hit_k, axis=1)
    lower = jnp.tril(jnp.ones((held, held), f32))
    rank = dot(lower, hit.astype(f32)).astype(jnp.int32) - 1
    slots = jnp.arange(cap, dtype=jnp.int32)
    pick = hit[:, :, None] & (rank[:, :, None] == slots)
    which = (lax.rem(expert_ids, E_NODE)[:, :, None] == jnp.arange(E_NODE)) & True
    named = hit_k[:, :, :, None] & which[:, :, None, :]
    weight = jnp.sum(jnp.where(named, gates.astype(f32)[:, :, None, None], 0.0), axis=1)
    rows = pick[:, 1:].astype(bf16)
    sel_t = jnp.einsum("trc,td->rcd", rows, tokens, preferred_element_type=f32).astype(bf16)
    sel_g = jnp.einsum("trc,td->rcd", rows, grad_out, preferred_element_type=f32).astype(bf16)
    slot_w = jnp.sum(jnp.where(pick[:, 1:, :, None], weight[:, 1:, None, :], 0.0), axis=0)
    meta = jnp.zeros((nodes, held, LANES), f32)
    meta = meta.at[0, :, :E_NODE].set(weight[:, 0])
    meta = meta.at[1:, :cap, :E_NODE].set(slot_w).astype(bf16)

    all_t, all_g, ext_t, ext_g, all_m = gather_rows(
        nodes, locals_,
        tokens.reshape(own_blocks, cap, width), grad_out.reshape(own_blocks, cap, width),
        sel_t, sel_g, meta,
    )
    total = locals_ * (held + (nodes - 1) * cap)
    rows_t, rows_g = all_t.reshape(total, width), all_g.reshape(total, width)
    units = s_gate.shape[1]

    def own(values):
        return values.reshape(locals_, -1, values.shape[-1])[:, :held].reshape(
            locals_ * held, values.shape[-1]
        )

    pre_gate, pre_up = dot(rows_t, s_gate), dot(rows_t, s_up)
    upstream = flip(dot(rows_g, s_down), locals_)
    sg, su, sh, _ = ffn_backward(own(pre_gate), own(pre_up), own(upstream), 1.0)
    pack = jnp.concatenate([sg, su, flip(sh, locals_)], axis=1)
    packs = [pack] + [
        lax.ppermute(pack, "node", [((i + s) % nodes, i) for i in range(nodes)])
        for s in range(1, nodes)
    ]

    expert = l // (locals_ // E_NODE)
    table = jnp.concatenate([all_m[0, :, :, :E_NODE]] + [
        all_m[s, :, :cap, :E_NODE] for s in range(1, nodes)
    ], axis=1).reshape(total, E_NODE).astype(f32)
    mine = jnp.arange(E_NODE) == expert
    row_w = jnp.sum(jnp.where(mine, table, 0.0), axis=1, keepdims=True)
    gate_w, up_w, down_w = w_gate[0], w_up[0], w_down[0]
    gg, gu, gh, product = ffn_backward(
        dot(rows_t, gate_w), dot(rows_t, up_w), flip(dot(rows_g, down_w), locals_), row_w
    )

    def widen(values):
        return jnp.pad(
            values.reshape(locals_, held, -1), ((0, 0), (0, (nodes - 1) * cap), (0, 0))
        ).reshape(total, -1)

    partial_dx = (
        contract_last(gg, gate_w) + contract_last(gu, up_w)
        + contract_last(widen(sg), s_gate) + contract_last(widen(su), s_up)
    ).astype(bf16)
    score = jnp.sum(product, axis=1, keepdims=True)
    lane = jnp.arange(LANES)
    score = jnp.where(lane == expert, score, 0.0).astype(bf16)
    part = jnp.concatenate([partial_dx, score], axis=1).reshape(
        locals_, own_blocks + nodes - 1, cap, width + LANES
    )
    own_sum, home = reduce_rows(nodes, locals_, part)

    expert_grads = tuple(
        g.astype(bf16)[None]
        for g in (contract_first(rows_t, gg), contract_first(rows_t, gu),
                  contract_first(rows_g, flip(gh, locals_)))
    )
    piece = width // nodes
    start = n * piece
    here_t = own(lax.dynamic_slice_in_dim(rows_t, start, piece, 1))
    here_g = own(lax.dynamic_slice_in_dim(rows_g, start, piece, 1))
    every_t = jnp.concatenate([here_t, ext_t.reshape(-1, piece)], axis=0)
    every_g = jnp.concatenate([here_g, ext_g.reshape(-1, piece)], axis=0)
    packed = jnp.concatenate(packs, axis=0)
    shared_grads = (
        contract_first(every_t, packed[:, :units]).astype(bf16),
        contract_first(every_t, packed[:, units : 2 * units]).astype(bf16),
        contract_first(every_g, packed[:, 2 * units :]).astype(bf16),
    )

    own_rows = own_sum.reshape(held, width + LANES).astype(f32)
    home_rows = jnp.einsum("trc,rcd->td", rows, home[:, :, :width], preferred_element_type=f32)
    dx = (own_rows[:, :width] + home_rows).astype(bf16)
    home_score = jnp.sum(
        jnp.where(pick[:, 1:, :, None], home[None, :, :, width : width + E_NODE].astype(f32), 0.0),
        axis=2,
    )
    scores = jnp.concatenate([own_rows[:, None, width : width + E_NODE], home_score], axis=1)
    dgates = jnp.sum(jnp.where(named, scores[:, None], 0.0), axis=(2, 3))
    return (dx, dgates) + expert_grads + shared_grads


def solution(mesh):
    token = P(("node", "local"), None)
    routed = P("node", None, "local")
    shared = P(None, "local")
    shared_out = P("node", "local")
    return jax.shard_map(
        local,
        mesh=mesh,
        in_specs=(token,) * 4 + (routed,) * 3 + (shared,) * 3,
        out_specs=(token,) * 2 + (routed,) * 3 + (shared_out,) * 3,
        check_vma=False,
    )
```

time: 375 us -> 182 us (0.49)
  waiting for transfers between devices: 181 us -> 0.01 us
  Pallas kernels: 0 us -> 101 us
  blocking collectives: 68.3 us -> 0 us
  starting transfers between devices: 27.8 us -> 10.4 us
  between operations: 14.1 us -> 1.06 us
  local copies, waits for them, and re-layouts: 15 us -> 6.96 us
  other arithmetic: 12.4 us -> 8.52 us
    all_to_all x7 -> x0, waiting for transfers between devices: 125 us -> none  [the longest x1 43 us: routed_part(): lax.all_to_all(spread(routed_in), 'local', split_axis=0, concat_axis=0, t...]
    pallas_call x0 -> x2, Pallas kernels: none -> 101 us  [the longest x1 64.8 us: gather_rows(): pl.pallas_call(functools.partial(gather_kernel, node_count, orders), out_...]
    all_to_all x4 -> x0, blocking collectives: 68.3 us -> none  [the longest x1 45.9 us: routed_part(): lax.all_to_all(partial_value.reshape(rows_in.shape), 'local', split_axis=...]
    all_gather x2 -> x0, waiting for transfers between devices: 54.3 us -> none  [the longest x1 30.6 us: shared_part(): lax.all_gather(tokens, 'local', axis=0, tiled=True)]
    all_to_all x7 -> x0, starting transfers between devices: 27.7 us -> none  [the longest x1 4.68 us: routed_part(): lax.all_to_all(spread(routed_grad), 'local', split_axis=0, concat_axis=0,...]
    ppermute x0 -> x3, starting transfers between devices: none -> 10.4 us  [local(): lax.ppermute(pack, 'node', [((i + s) % nodes, i) for i in range(nodes)])]
    dot_general x15 -> x10, matrix products: 28.2 us -> 20.6 us  [the longest x7 15.8 us: dot(): return jnp.dot(left, right, preferred_element_type=jnp.float32)]
    concatenate x1 -> x4, other arithmetic: 10.9 us -> 4.2 us  [the longest x1 2.42 us: local(): jnp.concatenate([partial_dx, score], axis=1)]
  transfers between devices with their start and end apart: 11 -> 3, of which waited for: 8 -> 0; matrix products, arithmetic and copies ran while one was open for 18% -> 25% of each run, Pallas kernels for 0% -> 20%
where the time goes in v1:
time: 182 us
  Pallas kernels  101 us (55%)
  matrix products  53.7 us (30%)
  starting transfers between devices  10.4 us (6%)
  other arithmetic  8.52 us (5%)
  local copies, waits for them, and re-layouts  6.96 us (4%)
    pallas_call x1, Pallas kernels, gather_rows(): pl.pallas_call(functools.partial(gather_kernel, node_count, orders), out_...  64.8 us
    pallas_call x1, Pallas kernels, reduce_rows(): pl.pallas_call(functools.partial(reduce_kernel, node_count, forward, own_...  36.4 us
    dot_general x6, matrix products, contract_first(): lax.dot_general(left, right, (((0,), (0,)), ((), ())), preferred_element_...  21.6 us
    dot_general x7, matrix products, dot(): return jnp.dot(left, right, preferred_element_type=jnp.float32)  15.8 us
    dot_general x4, matrix products, contract_last(): lax.dot_general(left, right, (((1,), (1,)), ((), ())), preferred_element_...  11.5 us
    ppermute x3, starting transfers between devices, local(): lax.ppermute(pack, 'node', [((i + s) % nodes, i) for i in range(nodes)])  10.4 us
    unnamed x32, local copies, waits for them, and re-layouts  3.73 us
  transfers between devices with their start and end apart: 3, of which 0 were waited for; matrix products, arithmetic and copies ran while one was open for 25% of the time, Pallas kernels for 20%

profile of v1, /device:TPU:0, one launch (start us, length us, event | category | flops | bytes accessed | tf_op | source)
XLA Modules:
  0.0 181.8 jit_solution(10681487779609410746)
XLA Ops:
  0.6 0.7 negate_select_fusion.3
  2.5 1.9 %convolution_convert_fusion.3.sel_g = bf16[3,8,7168]{2,1,0:T(8,128)(2,1)} fusion(bf16[16,7168]{1,0:T(8,128)(2,1)} %param.15, s32[16,4]{0,1:T(4,128)S(1)} %fusion.32, pred[16,4]{0,1:T(4,128)(4,1)S(1)} %get-tuple-element.46), kind=kOutput, calls=%fused_computation.10 | convolution fusion | flops 5678080 | bytes 573760 | tf_op jit(solution)/shard_map/trc,td->rcd/dot_general | solution.py:332
  4.4 1.9 %convolution_convert_fusion.4.sel_t = bf16[3,8,7168]{2,1,0:T(8,128)(2,1)} fusion(bf16[16,7168]{1,0:T(8,128)(2,1)} %param.14, s32[16,4]{0,1:T(4,128)S(1)} %fusion.32, pred[16,4]{0,1:T(4,128)(4,1)S(1)} %get-tuple-element.46), kind=kOutput, calls=%fused_computation.11 | convolution fusion | flops 5678080 | bytes 573760 | tf_op jit(solution)/shard_map/trc,td->rcd/dot_general | solution.py:331
  7.3 64.8 %gather_rows.1 = (bf16[8,5,8,7168]{3,2,1,0:T(8,128)(2,1)}, bf16[8,5,8,7168]{3,2,1,0:T(8,128)(2,1)}, bf16[3,8,2,8,1792]{4,3,2,1,0:T(8,128)(2,1)}, bf16[3,8,2,8,17...) custom-call(bf16[2,8,7168]{2,1,0:T(8,128)(2,1)} %bitcast.151, bf16[2,8,7168]{2,1,0:T(8,128)(2,1)} %bitcast.152, ...), custom_call_target="tpu_custom_call" | custom-call | tf_op jit(solution)/shard_map/gather_rows/pallas_call | solution.py:138
  72.2 3.4 %fusion.10 = f32[8,16,256]{2,1,0:T(8,128)S(1)} fusion(bf16[7168,256]{1,0:T(8,128)(2,1)} %param.21, bf16[8,40,7168]{2,1,0:T(8,128)(2,1)} %bitcast.164), kind=kOutput, calls=%fused_computation.20 | convolution fusion | flops 469762048 | bytes 5636096 | tf_op jit(solution)/shard_map/dot_general | solution.py:279
  75.8 2.3 %fusion.12 = f32[8,16,256]{2,1,0:T(8,128)S(1)} fusion(bf16[7168,256]{1,0:T(8,128)(2,1)S(1)} %copy-done.2, bf16[8,40,7168]{2,1,0:T(8,128)(2,1)} %bitcast.165), kind=kOutput, calls=%fused_computation.22 | convolution fusion | flops 469762048 | bytes 5636096 | tf_op jit(solution)/shard_map/dot_general | solution.py:279
  78.2 0.8 copy-done.7
  79.0 1.5 fusion.29
  80.8 0.7 pad_maximum_fusion.5
  81.5 2.0 %collective-permute-start = (bf16[128,768]{1,0:T(8,128)(2,1)}, bf16[128,768]{1,0:T(8,128)(2,1)S(1)}, u32[]{:S(2)}, u32[]{:S(2)}) collective-permute-start(bf16[128,768]{1,0:T(8,128)(2,1)} %pad_maximum_fusion.5), channel_id=1, source_target_pairs={{8,0},{16,8},{24,16},{0,24},{9,1},{17,9},{25,17},{1,25},{10,2},{18... | collective-permute-start | bytes 589832 | tf_op jit(solution)/shard_map/ppermute | solution.py:357
  83.5 8.3 %collective-permute-start.1 = (bf16[128,768]{1,0:T(8,128)(2,1)}, bf16[128,768]{1,0:T(8,128)(2,1)}, u32[]{:S(2)}, u32[]{:S(2)}) collective-permute-start(bf16[128,768]{1,0:T(8,128)(2,1)} %pad_maximum_fusion.5), channel_id=1, source_target_pairs={{16,0},{24,8},{0,16},{8,24},{17,1},{25,9},{1,17},{9,25},{18,2},{26... | collective-permute-start | bytes 589832 | tf_op jit(solution)/shard_map/ppermute | solution.py:357
  92.6 4.9 %fusion.26 = f32[2,2,2,40,256]{4,3,1,2,0:T(8,128)S(1)} fusion(bf16[2,2,2,40,7168]{4,3,2,1,0:T(8,128)(2,1)} %bitcast.160, bf16[1,7168,256]{2,1,0:T(8,128)(2,1)} %param.20), kind=kOutput, calls=%fused_computation.40 | convolution fusion | flops 1174405120 | bytes 8585216 | tf_op jit(solution)/shard_map/dot_general | solution.py:279
  97.6 0.7 slice-done.1
  98.3 1.4 fusion.16
  100.4 2.2 %multiply_convert_fusion = (bf16[320,256]{1,0:T(8,128)(2,1)}, bf16[320,256]{1,0:T(8,128)(2,1)S(1)}, bf16[320,256]{1,0:T(8,128)(2,1)S(1)}, bf16[320]{0:T(512)(128)(2,1)S(1)}) fusion(f32[320]{0:T(512)S(1)} %mul.86, f32[320,256]{1,0:T(8,128)S(1)} %fusion.16, f32[2,2,2,40,256]{4,3,2,1,0:T(8,128)S(1)} %copy.78, f32[320,256]{1,0:T(8,128)S(1)} %bitcast.159, ...), kind=kOutput, calls=%fused_computation.46 | convolution fusion | flops 1175961344 | bytes 9734016 | tf_op jit(solution)/shard_map/dot_general | solution.py:279
  102.5 4.9 %fusion.14 = f32[320,7168]{1,0:T(8,128)} fusion(bf16[320,256]{1,0:T(8,128)(2,1)S(1)} %get-tuple-element.49, bf16[1,7168,256]{2,1,0:T(8,128)(2,1)S(1)} %copy-done.1), kind=kOutput, calls=%fused_computation.24 | convolution fusion | flops 1174405120 | bytes 13008896 | tf_op jit(solution)/shard_map/dot_general | solution.py:289
  107.5 4.0 %fusion.1 = bf16[1,7168,256]{2,1,0:T(8,128)(2,1)} fusion(bf16[320,7168]{1,0:T(8,128)(2,1)S(1)} %bitcast.172, bf16[320,256]{1,0:T(8,128)(2,1)S(1)} %get-tuple-element.49), kind=kOutput, calls=%fused_computation.7 | convolution fusion | flops 1176240128 | bytes 8421376 | tf_op jit(solution)/shard_map/dot_general | solution.py:283
  111.4 1.8 constant_dynamic-slice_fusion
  113.3 6.4 %fusion.2 = bf16[1,7168,256]{2,1,0:T(8,128)(2,1)} fusion(bf16[320,7168]{1,0:T(8,128)(2,1)} %bitcast.167, bf16[320,256]{1,0:T(8,128)(2,1)S(1)} %get-tuple-element.50), kind=kOutput, calls=%fused_computation.8 | convolution fusion | flops 1176240128 | bytes 8421376 | tf_op jit(solution)/shard_map/dot_general | solution.py:283
  120.3 1.4 convolution_add_fusion.2
  121.7 3.8 %convolution_add_fusion.1 = f32[320,7168]{1,0:T(8,128)S(1)} fusion(f32[320,7168]{1,0:T(8,128)S(1)} %convolution_add_fusion.2, bf16[320,256]{1,0:T(8,128)(2,1)S(1)} %bitcast.149, bf16[7168,256]{1,0:T(8,128)(2,1)} %param.21), kind=kOutput, calls=%fused_computation.1 | convolution fusion | flops 1176698880 | bytes 22183936 | tf_op jit(solution)/shard_map/dot_general | solution.py:289
  125.6 1.4 fusion
  127.1 2.4 %pad_maximum_fusion = bf16[320,7296]{1,0:T(8,128)(2,1)} fusion(bf16[320,128]{1,0:T(8,128)(2,1)S(1)} %select_convert_fusion, bf16[320,7168]{1,0:T(8,128)(2,1)S(1)} %fusion), kind=kLoop, calls=%fused_computation.15 | loop fusion | flops 9338880 | bytes 9338880 | tf_op jit(solution)/shard_map/concatenate | solution.py:384
  129.5 36.4 %reduce_rows.1 = (bf16[2,8,7296]{2,1,0:T(8,128)(2,1)}, bf16[3,8,7296]{2,1,0:T(8,128)(2,1)}) custom-call(bf16[8,5,8,7296]{3,2,1,0:T(8,128)(2,1)} %bitcast.144), custom_call_target="tpu_custom_call" | custom-call | tf_op jit(solution)/shard_map/reduce_rows/pallas_call | solution.py:250
  165.9 1.0 bitcast_convert_fusion
  166.9 0.7 slice_convert_fusion
  168.5 6.4 %fusion.3 = bf16[1,7168,256]{2,1,0:T(8,128)(2,1)} fusion(bf16[320,7168]{1,0:T(8,128)(2,1)} %bitcast.162, bf16[320,256]{1,0:T(8,128)(2,1)S(1)} %bitcast.174), kind=kOutput, calls=%fused_computation.9 | convolution fusion | flops 1176240128 | bytes 8421376 | tf_op jit(solution)/shard_map/dot_general | solution.py:283
  174.9 1.0 fusion.5
  175.8 1.1 pad_maximum_fusion.4
  176.9 1.6 convolution_convert_fusion.6
  178.5 1.6 convolution_convert_fusion.7
  180.2 1.6 convolution_convert_fusion.5
  (78 shorter events, 5.7 us)
Async XLA Ops:
  6.7 0.6 copy-start.9
  72.1 3.7 %copy-start.2 = (bf16[7168,256]{1,0:T(8,128)(2,1)S(1)}, bf16[7168,256]{1,0:T(8,128)(2,1)}, u32[]{:S(2)}) copy-start(bf16[7168,256]{1,0:T(8,128)(2,1)} %param.22) | copy-start | bytes 11010052
  72.1 6.0 %copy-start.11 = (bf16[7168,256]{1,0:T(8,128)(2,1)S(1)}, bf16[7168,256]{1,0:T(8,128)(2,1)}, u32[]{:S(2)}) copy-start(bf16[7168,256]{1,0:T(8,128)(2,1)} %param.23) | copy-start | bytes 11010052
  75.8 3.2 %copy-start.7 = (bf16[8,5,8,7168]{3,2,1,0:T(8,128)(2,1)S(1)}, bf16[8,5,8,7168]{3,2,1,0:T(8,128)(2,1)}, u32[]{:S(2)}) copy-start(bf16[8,5,8,7168]{3,2,1,0:T(8,128)(2,1)} %get-tuple-element.40) | copy-start | bytes 13762564
  79.0 12.8 %copy-start.10 = (bf16[4,8,16,128]{3,2,1,0:T(8,128)(2,1)S(1)}, bf16[4,8,16,128]{3,2,1,0:T(8,128)(2,1)}, u32[]{:S(2)}) copy-start(bf16[4,8,16,128]{3,2,1,0:T(8,128)(2,1)} %get-tuple-element.39) | copy-start | bytes 393220
  80.8 16.8 %slice-start = ((s8[4587520]{0:T(1024)(128)(4,1)}), s8[393216]{0:T(1024)(128)(4,1)S(1)}, s32[]{:S(2)}) async-start(s8[4587520]{0:T(1024)(128)(4,1)} %bitcast.168), calls=%async_computation | async-start | bytes 786432
  81.5 94.4 %collective-permute-start = (bf16[128,768]{1,0:T(8,128)(2,1)}, bf16[128,768]{1,0:T(8,128)(2,1)S(1)}, u32[]{:S(2)}, u32[]{:S(2)}) collective-permute-start(bf16[128,768]{1,0:T(8,128)(2,1)} %pad_maximum_fusion.5), channel_id=1, source_target_pairs={{8,0},{16,8},{24,16},{0,24},{9,1},{17,9},{25,17},{1,25},{10,2},{18... | collective-permute-start | bytes 589832 | tf_op jit(solution)/shard_map/ppermute | solution.py:357
  83.5 92.3 %collective-permute-start.1 = (bf16[128,768]{1,0:T(8,128)(2,1)}, bf16[128,768]{1,0:T(8,128)(2,1)}, u32[]{:S(2)}, u32[]{:S(2)}) collective-permute-start(bf16[128,768]{1,0:T(8,128)(2,1)} %pad_maximum_fusion.5), channel_id=1, source_target_pairs={{16,0},{24,8},{0,16},{8,24},{17,1},{25,9},{1,17},{9,25},{18,2},{26... | collective-permute-start | bytes 589832 | tf_op jit(solution)/shard_map/ppermute | solution.py:357
  91.8 84.0 %collective-permute-start.2 = (bf16[128,768]{1,0:T(8,128)(2,1)}, bf16[128,768]{1,0:T(8,128)(2,1)}, u32[]{:S(2)}, u32[]{:S(2)}) collective-permute-start(bf16[128,768]{1,0:T(8,128)(2,1)} %pad_maximum_fusion.5), channel_id=1, source_target_pairs={{24,0},{0,8},{8,16},{16,24},{25,1},{1,9},{9,17},{17,25},{26,2},{2,... | collective-permute-start | bytes 589832 | tf_op jit(solution)/shard_map/ppermute | solution.py:357
  92.6 5.0 %copy-start.1 = (bf16[1,7168,256]{2,1,0:T(8,128)(2,1)S(1)}, bf16[1,7168,256]{2,1,0:T(8,128)(2,1)}, u32[]{:S(2)}) copy-start(bf16[1,7168,256]{2,1,0:T(8,128)(2,1)} %param.18) | copy-start | bytes 11010052
  92.6 5.7 %slice-start.1 = ((s8[4587520]{0:T(1024)(128)(4,1)}), s8[4194304]{0:T(1024)(128)(4,1)S(1)}, s32[]{:S(2)}) async-start(s8[4587520]{0:T(1024)(128)(4,1)} %bitcast.168), calls=%async_computation.1 | async-start | bytes 8388608
  98.3 2.0 %copy-start.4 = (bf16[1,7168,256]{2,1,0:T(8,128)(2,1)S(1)}, bf16[1,7168,256]{2,1,0:T(8,128)(2,1)}, u32[]{:S(2)}) copy-start(bf16[1,7168,256]{2,1,0:T(8,128)(2,1)} %param.19) | copy-start | bytes 11010052
  113.2 6.5 %copy-start.5 = (bf16[1,7168,256]{2,1,0:T(8,128)(2,1)S(1)}, bf16[1,7168,256]{2,1,0:T(8,128)(2,1)}, u32[]{:S(2)}) copy-start(bf16[1,7168,256]{2,1,0:T(8,128)(2,1)} %param.19) | copy-start | bytes 11010052
  113.3 7.0 %copy-start = (f32[320,7168]{1,0:T(8,128)S(1)}, f32[320,7168]{1,0:T(8,128)}, u32[]{:S(2)}) copy-start(f32[320,7168]{1,0:T(8,128)} %fusion.14) | copy-start | bytes 27525124
  121.7 3.8 %copy-start.3 = (bf16[7168,256]{1,0:T(8,128)(2,1)S(1)}, bf16[7168,256]{1,0:T(8,128)(2,1)}, u32[]{:S(2)}) copy-start(bf16[7168,256]{1,0:T(8,128)(2,1)} %param.22) | copy-start | bytes 11010052
  129.5 39.0 %copy-start.8 = (bf16[320,256]{1,0:T(8,128)(2,1)S(1)}, bf16[320,256]{1,0:T(8,128)(2,1)}, u32[]{:S(2)}) copy-start(bf16[320,256]{1,0:T(8,128)(2,1)} %get-tuple-element.48) | copy-start | bytes 491524
  168.5 6.4 %copy-start.6 = (bf16[3,8,7296]{2,1,0:T(8,128)(2,1)S(1)}, bf16[3,8,7296]{2,1,0:T(8,128)(2,1)}, u32[]{:S(2)}) copy-start(bf16[3,8,7296]{2,1,0:T(8,128)(2,1)} %get-tuple-element.43) | copy-start | bytes 1050628
  168.5 8.4 %copy-start.13 = (bf16[3,8,2,8,1792]{4,3,2,1,0:T(8,128)(2,1)S(1)}, bf16[3,8,2,8,1792]{4,3,2,1,0:T(8,128)(2,1)}, u32[]{:S(2)}) copy-start(bf16[3,8,2,8,1792]{4,3,2,1,0:T(8,128)(2,1)} %get-tuple-element.44) | copy-start | bytes 4128772
  178.5 1.6 copy-start.12

commit v2 on v1

--- a/solution.py
+++ b/solution.py
@@ -156,16 +156,50 @@
     )(tok, grad, sel_t, sel_g, meta)
 
 
-def reduce_kernel(node_count, forward, own_blocks, part_ref, own_ref, home_ref,
-                  acc, land, back, send_sem, recv_sem, zsend_sem, zrecv_sem, load_sem):
+def reduce_kernel(node_count, forward, own_blocks, part_ref, rows_t, rows_g, gg, gu, gh, pack,
+                  own_ref, home_ref, packs, dw_g, dw_u, dw_d,
+                  acc, land, back, held_t, held_g, grads,
+                  send_sem, recv_sem, zsend_sem, zrecv_sem, psend_sem, precv_sem, load_sem, out_sem):
     n, l = lax.axis_index("node"), lax.axis_index("local")
     count, blocks, cap, width = part_ref.shape
     stages = len(forward)
     half = width // 2 // LANES * LANES
-    load = pltpu.make_async_copy(part_ref, acc, load_sem)
+    load = pltpu.make_async_copy(part_ref, acc, load_sem.at[0])
     load.start()
+    load_t = pltpu.make_async_copy(rows_t, held_t, load_sem.at[1])
+    load_t.start()
+    load_g = pltpu.make_async_copy(rows_g, held_g, load_sem.at[2])
+    load_g.start()
     greet(node_count, forward)
+    passed = []
+    for s in near_first(node_count):
+        copy = pltpu.make_async_remote_copy(
+            src_ref=pack, dst_ref=packs.at[node_count - s - 1],
+            send_sem=psend_sem.at[s - 1], recv_sem=precv_sem.at[node_count - s - 1],
+            device_id=(lax.rem(n + s, node_count), l), device_id_type=MESH,
+        )
+        copy.start()
+        passed.append(copy)
     load.wait()
+    tile = 4 * LANES
+    work = [(load_t, held_t, gg, dw_g), (None, held_t, gu, dw_u), (load_g, held_g, gh, dw_d)]
+    stored = []
+
+    def multiply(index):
+        ready, held, right, out = work[index]
+        if ready is not None:
+            ready.wait()
+
+        def step(c, carry):
+            at = pl.ds(pl.multiple_of(c * tile, tile), tile)
+            grads[index, at, :] = contract_first(held[:, at], right[...]).astype(jnp.bfloat16)
+            return carry
+
+        lax.fori_loop(0, held.shape[1] // tile, step, 0)
+        copy = pltpu.make_async_copy(grads.at[index], out, out_sem.at[index])
+        copy.start()
+        stored.append(copy)
+
     groups = [(own_blocks, blocks - own_blocks), (0, own_blocks)]
     bands = [(0, half), (half, width - half)]
     top = stages - 1
@@ -232,42 +266,59 @@
                     )
                     copy.start()
                     homes.append(copy)
+        if stage < len(work):
+            multiply(stage)
+    for index in range(stages + 1, len(work)):
+        multiply(index)
     own_ref[...] = acc[0, pl.ds(0, own_blocks)]
     for copy in homes:
         copy.wait_recv()
     home_ref[...] = back[...]
-    for copy in sends + homes:
+    for copy in passed:
+        copy.wait_recv()
+    for copy in sends + homes + passed:
         copy.wait_send()
-
-
-def reduce_rows(node_count, local_count, part):
+    for copy in stored:
+        copy.wait()
+
+
+def reduce_rows(node_count, local_count, part, rows_t, rows_g, gg, gu, gh, pack):
     count, blocks, cap, width = part.shape
     forward = bit_orders(local_count)[0]
     own_blocks = blocks - (node_count - 1)
     bf16 = jnp.bfloat16
     vmem = pl.BlockSpec(memory_space=pltpu.VMEM)
+    hbm = pl.BlockSpec(memory_space=pl.ANY)
     copies = 4 * (local_count - 1)
+    grad = (rows_t.shape[1], gg.shape[1])
     return pl.pallas_call(
         functools.partial(reduce_kernel, node_count, forward, own_blocks),
         out_shape=[
             jax.ShapeDtypeStruct((own_blocks, cap, width), bf16),
             jax.ShapeDtypeStruct((node_count - 1, cap, width), bf16),
-        ],
-        in_specs=[pl.BlockSpec(memory_space=pl.ANY)],
-        out_specs=[vmem] * 2,
+            jax.ShapeDtypeStruct((node_count - 1,) + pack.shape, bf16),
+        ] + [jax.ShapeDtypeStruct(grad, bf16)] * 3,
+        in_specs=[hbm] * 3 + [vmem] * 4,
+        out_specs=[vmem] * 2 + [hbm] * 4,
         scratch_shapes=[
             pltpu.VMEM(part.shape, bf16),
             pltpu.VMEM(part.shape, bf16),
             pltpu.VMEM((node_count - 1, cap, width), bf16),
+            pltpu.VMEM(rows_t.shape, bf16),
+            pltpu.VMEM(rows_g.shape, bf16),
+            pltpu.VMEM((3,) + grad, bf16),
             pltpu.SemaphoreType.DMA((copies,)),
             pltpu.SemaphoreType.DMA((copies,)),
             pltpu.SemaphoreType.DMA((node_count - 1,)),
             pltpu.SemaphoreType.DMA((node_count - 1,)),
-            pltpu.SemaphoreType.DMA,
+            pltpu.SemaphoreType.DMA((node_count - 1,)),
+            pltpu.SemaphoreType.DMA((node_count - 1,)),
+            pltpu.SemaphoreType.DMA((3,)),
+            pltpu.SemaphoreType.DMA((3,)),
         ],
         compiler_params=pltpu.CompilerParams(collective_id=1, has_side_effects=True),
         name="reduce_rows",
-    )(part)
+    )(part, rows_t, rows_g, gg, gu, gh, pack)
 
 
 def silu_parts(pre_gate):
@@ -353,11 +404,6 @@
     upstream = flip(dot(rows_g, s_down), locals_)
     sg, su, sh, _ = ffn_backward(own(pre_gate), own(pre_up), own(upstream), 1.0)
     pack = jnp.concatenate([sg, su, flip(sh, locals_)], axis=1)
-    packs = [pack] + [
-        lax.ppermute(pack, "node", [((i + s) % nodes, i) for i in range(nodes)])
-        for s in range(1, nodes)
-    ]
-
     expert = l // (locals_ // E_NODE)
     table = jnp.concatenate([all_m[0, :, :, :E_NODE]] + [
         all_m[s, :, :cap, :E_NODE] for s in range(1, nodes)
@@ -384,20 +430,17 @@
     part = jnp.concatenate([partial_dx, score], axis=1).reshape(
         locals_, own_blocks + nodes - 1, cap, width + LANES
     )
-    own_sum, home = reduce_rows(nodes, locals_, part)
-
-    expert_grads = tuple(
-        g.astype(bf16)[None]
-        for g in (contract_first(rows_t, gg), contract_first(rows_t, gu),
-                  contract_first(rows_g, flip(gh, locals_)))
-    )
+    own_sum, home, packs, *dw = reduce_rows(
+        nodes, locals_, part, rows_t, rows_g, gg, gu, flip(gh, locals_), pack
+    )
+    expert_grads = tuple(g[None] for g in dw)
     piece = width // nodes
     start = n * piece
     here_t = own(lax.dynamic_slice_in_dim(rows_t, start, piece, 1))
     here_g = own(lax.dynamic_slice_in_dim(rows_g, start, piece, 1))
     every_t = jnp.concatenate([here_t, ext_t.reshape(-1, piece)], axis=0)
     every_g = jnp.concatenate([here_g, ext_g.reshape(-1, piece)], axis=0)
-    packed = jnp.concatenate(packs, axis=0)
+    packed = jnp.concatenate([pack, packs.reshape(-1, pack.shape[1])], axis=0)
     shared_grads = (
         contract_first(every_t, packed[:, :units]).astype(bf16),
         contract_first(every_t, packed[:, units : 2 * units]).astype(bf16),

time: 182 us -> 175 us (0.962)
  matrix products: 53.7 us -> 38.4 us
  Pallas kernels: 101 us -> 112 us
  starting transfers between devices: 10.4 us -> 0 us
  local copies, waits for them, and re-layouts: 6.96 us -> 14.8 us
    dot_general x6 -> x3, matrix products: 21.6 us -> 6.29 us  [contract_first(): lax.dot_general(left, right, (((0,), (0,)), ((), ())), preferred_element_...]
    pallas_call x1, Pallas kernels: 36.4 us -> 47.1 us  [reduce_rows(): pl.pallas_call(functools.partial(reduce_kernel, node_count, forward, own_...]
    ppermute x3 -> x0, starting transfers between devices: 10.4 us -> none  [local(): lax.ppermute(pack, 'node', [((i + s) % nodes, i) for i in range(nodes)])]
    unnamed x32 -> x53, local copies, waits for them, and re-layouts: 3.73 us -> 10.9 us
    dot_general x7, matrix products: 15.8 us -> 19.3 us  [dot(): return jnp.dot(left, right, preferred_element_type=jnp.float32)]
    dot_general x4, matrix products: 11.5 us -> 8.02 us  [contract_last(): lax.dot_general(left, right, (((1,), (1,)), ((), ())), preferred_element_...]
  transfers between devices with their start and end apart: 3 -> 0, of which waited for: 0 -> 0; matrix products, arithmetic and copies ran while one was open for 25% -> 0% of each run, Pallas kernels for 20% -> 0%
where the time goes in v2:
time: 175 us; the launch traced here: 174 us
  Pallas kernels  112 us (64%)
  matrix products  38.4 us (22%)
  local copies, waits for them, and re-layouts  14.8 us (8%)
  other arithmetic  7.54 us (4%)
    pallas_call x1, Pallas kernels, gather_rows(): pl.pallas_call(functools.partial(gather_kernel, node_count, orders), out_...  64.9 us
    pallas_call x1, Pallas kernels, reduce_rows(): pl.pallas_call(functools.partial(reduce_kernel, node_count, forward, own_...  47.1 us
    dot_general x7, matrix products, dot(): return jnp.dot(left, right, preferred_element_type=jnp.float32)  19.3 us
    unnamed x53, local copies, waits for them, and re-layouts  10.9 us
    dot_general x4, matrix products, contract_last(): lax.dot_general(left, right, (((1,), (1,)), ((), ())), preferred_element_...  8.02 us
    dot_general x3, matrix products, contract_first(): lax.dot_general(left, right, (((0,), (0,)), ((), ())), preferred_element_...  6.29 us

profile of v2, /device:TPU:0, one launch (start us, length us, event | category | flops | bytes accessed | tf_op | source)
XLA Modules:
  0.0 173.8 jit_solution(12360530901470655045)
XLA Ops:
  0.6 0.7 negate_select_fusion.3
  1.5 0.7 convert_element_type.80
  2.9 1.9 %convolution_convert_fusion.sel_g = bf16[3,8,7168]{2,1,0:T(8,128)(2,1)} fusion(bf16[16,7168]{1,0:T(8,128)(2,1)} %param.15, s32[16,4]{0,1:T(4,128)S(1)} %fusion.29, pred[16,4]{0,1:T(4,128)(4,1)S(1)} %get-tuple-element.54), kind=kOutput, calls=%fused_computation.4 | convolution fusion | flops 5678080 | bytes 573760 | tf_op jit(solution)/shard_map/trc,td->rcd/dot_general | solution.py:383
  4.8 1.9 %convolution_convert_fusion.1.sel_t = bf16[3,8,7168]{2,1,0:T(8,128)(2,1)} fusion(bf16[16,7168]{1,0:T(8,128)(2,1)} %param.14, s32[16,4]{0,1:T(4,128)S(1)} %fusion.29, pred[16,4]{0,1:T(4,128)(4,1)S(1)} %get-tuple-element.54), kind=kOutput, calls=%fused_computation.5 | convolution fusion | flops 5678080 | bytes 573760 | tf_op jit(solution)/shard_map/trc,td->rcd/dot_general | solution.py:382
  6.7 64.9 %gather_rows.1 = (bf16[8,5,8,7168]{3,2,1,0:T(8,128)(2,1)}, bf16[8,5,8,7168]{3,2,1,0:T(8,128)(2,1)}, bf16[3,8,2,8,1792]{4,3,2,1,0:T(8,128)(2,1)}, bf16[3,8,2,8,17...) custom-call(bf16[2,8,7168]{2,1,0:T(8,128)(2,1)} %bitcast.158, bf16[2,8,7168]{2,1,0:T(8,128)(2,1)} %bitcast.159, ...), custom_call_target="tpu_custom_call" | custom-call | tf_op jit(solution)/shard_map/gather_rows/pallas_call | solution.py:138
  71.6 3.4 %fusion.7 = f32[8,16,256]{2,1,0:T(8,128)S(1)} fusion(bf16[7168,256]{1,0:T(8,128)(2,1)} %param.21, bf16[8,40,7168]{2,1,0:T(8,128)(2,1)} %bitcast.137), kind=kOutput, calls=%fused_computation.14 | convolution fusion | flops 469762048 | bytes 5636096 | tf_op jit(solution)/shard_map/dot_general | solution.py:330
  75.5 2.9 %fusion.9 = f32[8,16,256]{2,1,0:T(8,128)S(1)} fusion(bf16[7168,256]{1,0:T(8,128)(2,1)} %param.22, bf16[8,40,7168]{2,1,0:T(8,128)(2,1)S(1)} %bitcast.141), kind=kOutput, calls=%fused_computation.16 | convolution fusion | flops 469762048 | bytes 5636096 | tf_op jit(solution)/shard_map/dot_general | solution.py:330
  78.4 0.8 copy-done.1
  79.2 1.5 fusion.26
  80.8 0.7 multiply_convert_fusion.3
  81.7 0.7 pad_maximum_fusion.5.pack
  83.1 4.9 %fusion.13 = f32[320,256]{1,0:T(8,128)S(1)} fusion(bf16[320,7168]{1,0:T(8,128)(2,1)} %bitcast.138, bf16[1,7168,256]{2,1,0:T(8,128)(2,1)} %param.18), kind=kOutput, calls=%fused_computation.20 | convolution fusion | flops 1174405120 | bytes 8585216 | tf_op jit(solution)/shard_map/dot_general | solution.py:330
  88.1 3.8 %fusion.23 = f32[2,2,2,40,256]{4,3,1,2,0:T(8,128)S(1)} fusion(bf16[2,2,2,40,7168]{4,3,2,1,0:T(8,128)(2,1)} %bitcast.145, bf16[1,7168,256]{2,1,0:T(8,128)(2,1)S(1)} %copy-done.21), kind=kOutput, calls=%fused_computation.34 | convolution fusion | flops 1174405120 | bytes 8585216 | tf_op jit(solution)/shard_map/dot_general | solution.py:330
  92.0 2.7 %multiply_convert_fusion = (bf16[320,256]{1,0:T(8,128)(2,1)}, bf16[320,256]{1,0:T(8,128)(2,1)S(1)}, bf16[320,256]{1,0:T(8,128)(2,1)S(1)}, bf16[320]{0:T(512)(128)(2,1)}) fusion(f32[320]{0:T(512)S(1)} %mul.86, f32[320,256]{1,0:T(8,128)S(1)} %fusion.13, f32[2,2,2,40,256]{4,3,2,1,0:T(8,128)S(1)} %copy.83, f32[320,256]{1,0:T(8,128)S(1)} %bitcast.168, ...), kind=kOutput, calls=%fused_computation.40 | convolution fusion | flops 1175961344 | bytes 9734016 | tf_op jit(solution)/shard_map/dot_general | solution.py:330
  94.7 1.4 fusion.11
  96.1 1.4 convolution_add_fusion.2
  97.5 3.6 %convolution_add_fusion.1 = f32[320,7168]{1,0:T(8,128)S(1)} fusion(f32[320,7168]{1,0:T(8,128)S(1)} %convolution_add_fusion.2, bf16[320,256]{1,0:T(8,128)(2,1)S(1)} %bitcast.156, bf16[7168,256]{1,0:T(8,128)(2,1)} %param.21), kind=kOutput, calls=%fused_computation.1 | convolution fusion | flops 1176698880 | bytes 22183936 | tf_op jit(solution)/shard_map/dot_general | solution.py:340
  101.2 1.6 fusion
  103.0 2.4 %pad_maximum_fusion = bf16[320,7296]{1,0:T(8,128)(2,1)} fusion(bf16[320,128]{1,0:T(8,128)(2,1)S(1)} %select_convert_fusion, bf16[320,7168]{1,0:T(8,128)(2,1)S(1)} %fusion), kind=kLoop, calls=%fused_computation.9 | loop fusion | flops 9338880 | bytes 9338880 | tf_op jit(solution)/shard_map/concatenate | solution.py:430
  105.4 0.7 copy.85
  106.1 47.1 %reduce_rows.1 = (bf16[2,8,7296]{2,1,0:T(8,128)(2,1)}, bf16[3,8,7296]{2,1,0:T(8,128)(2,1)}, bf16[3,128,768]{2,1,0:T(8,128)(2,1)}, bf16[7168,256]{1,0:T(8,128)(2,...) custom-call(bf16[8,5,8,7296]{3,2,1,0:T(8,128)(2,1)} %bitcast.136, bf16[320,7168]{1,0:T(8,128)(2,1)} %bitcast.139, ...), custom_call_target="tpu_custom_call" | custom-call | tf_op jit(solution)/shard_map/reduce_rows/pallas_call | solution.py:294
  153.2 1.1 pad_maximum_fusion.4
  154.3 1.8 %constant_dynamic-slice_fusion = (bf16[320,1792]{1,0:T(8,128)(2,1)S(1)}, bf16[320,1792]{1,0:T(8,128)(2,1)S(1)}) fusion(bf16[320,7168]{1,0:T(8,128)(2,1)} %bitcast.147, s32[]{:T(128)S(6)} %select_n.52, bf16[320,7168]{1,0:T(8,128)(2,1)} %bitcast.140), kind=kLoop, calls=%fused_computation.102 | loop fusion | bytes 4587524 | tf_op jit(solution)/shard_map/dynamic_slice | solution.py:440
  156.1 3.1 %convolution_convert_fusion.2 = bf16[1792,256]{1,0:T(8,128)(2,1)} fusion(bf16[384,1792]{1,0:T(8,128)(2,1)} %bitcast.177, bf16[128,1792]{1,0:T(8,128)(2,1)S(1)} %bitcast.167, bf16[512,768]{1,0:T(8,128)(2,1)S(1)} %pad_maximum_fusion.4), kind=kOutput, calls=%fused_computation.25 | convolution fusion | flops 473890816 | bytes 3014656 | tf_op jit(solution)/shard_map/dot_general | solution.py:334
  159.2 1.6 convolution_convert_fusion.3
  160.8 1.6 convolution_convert_fusion.4
  162.8 0.6 fusion.49
  163.4 1.0 fusion.2
  164.3 4.3 %copy.102 = bf16[1,7168,256]{2,1,0:T(8,128)(2,1)} copy(bf16[1,7168,256]{2,1,0:T(8,128)(2,1)} %bitcast.151) | data formatting | bytes 7340032
  168.6 1.9 %copy.103 = bf16[1,7168,256]{2,1,0:T(8,128)(2,1)} copy(bf16[1,7168,256]{2,1,0:T(8,128)(2,1)S(1)} %bitcast.150) | data formatting | bytes 7340032
  170.5 1.5 copy-done.4
  172.0 1.8 %copy.104 = bf16[1,7168,256]{2,1,0:T(8,128)(2,1)} copy(bf16[1,7168,256]{2,1,0:T(8,128)(2,1)S(1)} %bitcast.149) | data formatting | bytes 7340032
  (90 shorter events, 2.8 us)
Async XLA Ops:
  2.9 3.8 %copy-start.17 = (bf16[4,16,128]{2,1,0:T(8,128)(2,1)}, bf16[4,16,128]{2,1,0:T(8,128)(2,1)S(1)}, u32[]{:S(2)}) copy-start(bf16[4,16,128]{2,1,0:T(8,128)(2,1)S(1)} %scatter.9.meta) | copy-start | bytes 49156
  71.5 3.9 %copy-start = (bf16[8,5,8,7168]{3,2,1,0:T(8,128)(2,1)S(1)}, bf16[8,5,8,7168]{3,2,1,0:T(8,128)(2,1)}, u32[]{:S(2)}) copy-start(bf16[8,5,8,7168]{3,2,1,0:T(8,128)(2,1)} %get-tuple-element.45) | copy-start | bytes 13762564
  71.6 6.8 %copy-start.20 = (bf16[7168,256]{1,0:T(8,128)(2,1)S(1)}, bf16[7168,256]{1,0:T(8,128)(2,1)}, u32[]{:S(2)}) copy-start(bf16[7168,256]{1,0:T(8,128)(2,1)} %param.23) | copy-start | bytes 11010052
  75.5 3.8 %copy-start.1 = (bf16[8,5,8,7168]{3,2,1,0:T(8,128)(2,1)S(1)}, bf16[8,5,8,7168]{3,2,1,0:T(8,128)(2,1)}, u32[]{:S(2)}) copy-start(bf16[8,5,8,7168]{3,2,1,0:T(8,128)(2,1)} %get-tuple-element.44) | copy-start | bytes 13762564
  79.2 3.2 %copy-start.18 = (bf16[4,8,16,128]{3,2,1,0:T(8,128)(2,1)S(1)}, bf16[4,8,16,128]{3,2,1,0:T(8,128)(2,1)}, u32[]{:S(2)}) copy-start(bf16[4,8,16,128]{3,2,1,0:T(8,128)(2,1)} %get-tuple-element.43) | copy-start | bytes 393220
  81.6 6.5 %copy-start.9 = (bf16[128,256]{1,0:T(8,128)(2,1)}, bf16[128,256]{1,0:T(8,128)(2,1)S(1)}, u32[]{:S(2)}) copy-start(bf16[128,256]{1,0:T(8,128)(2,1)S(1)} %get-tuple-element.63) | copy-start | bytes 196612
  81.6 6.5 %copy-start.11 = (bf16[128,256]{1,0:T(8,128)(2,1)}, bf16[128,256]{1,0:T(8,128)(2,1)S(1)}, u32[]{:S(2)}) copy-start(bf16[128,256]{1,0:T(8,128)(2,1)S(1)} %get-tuple-element.64) | copy-start | bytes 196612
  81.6 10.3 %slice-start = ((s8[4587520]{0:T(1024)(128)(4,1)}), s8[393216]{0:T(1024)(128)(4,1)S(1)}, s32[]{:S(2)}) async-start(s8[4587520]{0:T(1024)(128)(4,1)} %bitcast.142), calls=%async_computation | async-start | bytes 786432
  83.1 5.0 %copy-start.21 = (bf16[1,7168,256]{2,1,0:T(8,128)(2,1)S(1)}, bf16[1,7168,256]{2,1,0:T(8,128)(2,1)}, u32[]{:S(2)}) copy-start(bf16[1,7168,256]{2,1,0:T(8,128)(2,1)} %param.20) | copy-start | bytes 11010052
  83.1 8.8 %slice-start.1 = ((s8[4587520]{0:T(1024)(128)(4,1)}), s8[4194304]{0:T(1024)(128)(4,1)S(1)}, s32[]{:S(2)}) async-start(s8[4587520]{0:T(1024)(128)(4,1)} %bitcast.142), calls=%async_computation.1 | async-start | bytes 8388608
  88.1 3.9 %copy-start.6 = (bf16[1,7168,256]{2,1,0:T(8,128)(2,1)S(1)}, bf16[1,7168,256]{2,1,0:T(8,128)(2,1)}, u32[]{:S(2)}) copy-start(bf16[1,7168,256]{2,1,0:T(8,128)(2,1)} %param.19) | copy-start | bytes 11010052
  92.0 2.7 %copy-start.2 = (bf16[1,7168,256]{2,1,0:T(8,128)(2,1)S(1)}, bf16[1,7168,256]{2,1,0:T(8,128)(2,1)}, u32[]{:S(2)}) copy-start(bf16[1,7168,256]{2,1,0:T(8,128)(2,1)} %param.18) | copy-start | bytes 11010052
  94.7 1.4 copy-start.8
  94.7 1.4 copy-start.7
  97.5 3.7 %copy-start.14 = (bf16[8,16,256]{2,1,0:T(8,128)(2,1)S(1)}, bf16[8,16,256]{2,1,0:T(8,128)(2,1)}, u32[]{:S(2)}) copy-start(bf16[8,16,256]{2,1,0:T(8,128)(2,1)} %get-tuple-element.60) | copy-start | bytes 196612
  97.5 3.7 %copy-start.3 = (bf16[7168,256]{1,0:T(8,128)(2,1)S(1)}, bf16[7168,256]{1,0:T(8,128)(2,1)}, u32[]{:S(2)}) copy-start(bf16[7168,256]{1,0:T(8,128)(2,1)} %param.22) | copy-start | bytes 11010052
  101.2 1.6 copy-start.19
  102.9 2.4 %copy-start.16 = (bf16[320,256]{1,0:T(8,128)(2,1)S(1)}, bf16[320,256]{1,0:T(8,128)(2,1)}, u32[]{:S(2)}) copy-start(bf16[320,256]{1,0:T(8,128)(2,1)} %get-tuple-element.56) | copy-start | bytes 491524
  106.1 47.1 %copy-start.10 = (bf16[128,256]{1,0:T(8,128)(2,1)S(1)}, bf16[128,256]{1,0:T(8,128)(2,1)}, u32[]{:S(2)}) copy-start(bf16[128,256]{1,0:T(8,128)(2,1)} %copy-done.9) | copy-start | bytes 196612
  106.1 47.1 %copy-start.12 = (bf16[128,256]{1,0:T(8,128)(2,1)S(1)}, bf16[128,256]{1,0:T(8,128)(2,1)}, u32[]{:S(2)}) copy-start(bf16[128,256]{1,0:T(8,128)(2,1)} %copy-done.11) | copy-start | bytes 196612
  156.0 3.1 %copy-start.22 = (bf16[3,8,2,8,1792]{4,3,2,1,0:T(8,128)(2,1)S(1)}, bf16[3,8,2,8,1792]{4,3,2,1,0:T(8,128)(2,1)}, u32[]{:S(2)}) copy-start(bf16[3,8,2,8,1792]{4,3,2,1,0:T(8,128)(2,1)} %get-tuple-element.51) | copy-start | bytes 4128772
  160.8 1.6 copy-start.15
  160.8 1.8 %copy-start.13 = (bf16[3,8,7296]{2,1,0:T(8,128)(2,1)S(1)}, bf16[3,8,7296]{2,1,0:T(8,128)(2,1)}, u32[]{:S(2)}) copy-start(bf16[3,8,7296]{2,1,0:T(8,128)(2,1)} %get-tuple-element.47) | copy-start | bytes 1050628
  164.3 4.3 %copy-start.5 = (bf16[7168,256]{1,0:T(8,128)(2,1)S(1)}, bf16[7168,256]{1,0:T(8,128)(2,1)}, u32[]{:S(2)}) copy-start(bf16[7168,256]{1,0:T(8,128)(2,1)} %get-tuple-element.49) | copy-start | bytes 11010052
  168.6 3.4 %copy-start.4 = (bf16[7168,256]{1,0:T(8,128)(2,1)S(1)}, bf16[7168,256]{1,0:T(8,128)(2,1)}, u32[]{:S(2)}) copy-start(bf16[7168,256]{1,0:T(8,128)(2,1)} %get-tuple-element.50) | copy-start | bytes 11010052
